TPU v7x, 32 devices: a whole 2x2x4 slice. The times are simulated.
32 devices in a mesh: section: 4 (over y, core), expert: 2 (over x), tensor: 4 (over z).
Axes of the slice: x: 2, y: 2, z: 4, core: 2. Of those that a mesh axis runs over, the one named last changes fastest.
Arguments:
- branch_weights: bfloat16 [2, 8192, 8192], P('expert', ('section', 'tensor')), may hold values from -0.125 to 0.125
- branch_gains: float32 [2, 8192], P('expert', ('section', 'tensor')), may hold values from 0.1 to 1.9
- column_order: int32 [2, 8192], P('expert'), may hold values from 0 to 8191, each once within a row
- layer_order: int32 [4], replicated, may hold values from 0 to 3, each once
- probe_seeds: int32 [1024], replicated, may hold values from 1 to 32767
Outputs:
- expert_weights: bfloat16 [2, 8192, 8192], P('expert', None, ('section', 'tensor'))
- checksum: float32 [2, 1024, 8192], P('expert', None, ('section', 'tensor'))
- fingerprint: float32 [2, 1024], P('expert')
- shared_gain: float32 [8192], replicated
Inputs may be any that keep to these rules, and one draw needn't show every extreme that they name: Each row of column_order names every hidden unit once. layer_order names every layer once.
All inputs are finite; a program needn't handle non-finite values.
Results may differ from a plain program's by a relative error of at most 0.0034.
Values may be sent and summed in bfloat16 or wider, within the bound.
A program may use at most 64 MiB of HBM per device.

v0:
```python
import jax
import jax.numpy as jnp
from jax import lax
from jax.sharding import PartitionSpec as P

D = 2048
FF = 8192


def probe_at(probe_seeds, row_ids):
    hashed = probe_seeds[:, None] * (row_ids[None, :] + 1) % 65521
    return (hashed % 511 - 255).astype(jnp.float32) / 256.0


def sketch(natural, probe_seeds):
    segment_rows = D // 2
    running = jnp.zeros((probe_seeds.shape[0], natural.shape[1]), jnp.float32)
    for portion in range(natural.shape[0] // segment_rows):
        row_ids = portion * segment_rows + lax.iota(jnp.int32, segment_rows)
        probes = probe_at(probe_seeds, row_ids).astype(jnp.bfloat16)
        running = running + jnp.dot(
            probes,
            natural[portion * segment_rows : (portion + 1) * segment_rows],
            preferred_element_type=jnp.float32,
        )
    return running


def local(branch_weights, branch_gains, column_order, layer_order, probe_seeds):
    weights = branch_weights[0]
    rows_dev = weights.shape[0]
    n_section = lax.axis_size("section")
    n_tensor = lax.axis_size("tensor")
    groups = n_section * n_tensor
    cols_dev = weights.shape[1] // groups
    layers = layer_order.shape[0]
    own_gains = branch_gains[0]
    mean_gains = lax.psum(own_gains, "expert") / lax.axis_size("expert")
    scaling = own_gains / mean_gains
    permuted = jnp.take(weights, column_order[0], axis=1)
    folded = (permuted.astype(jnp.float32) * scaling[:, None]).astype(jnp.bfloat16)
    per_layer = D // rows_dev
    slot_ids = lax.iota(jnp.int32, layers)
    inverse = jnp.sum(
        jnp.where(layer_order[None, :] == slot_ids[:, None], slot_ids[None, :], 0), axis=1
    )
    block_ids = lax.iota(jnp.int32, groups)
    layer_ids = block_ids // per_layer
    source_pos = (
        jnp.sum(jnp.where(layer_ids[:, None] == slot_ids[None, :], inverse[None, :], 0), axis=1)
        * per_layer
        + block_ids % per_layer
    )
    all_gains = lax.all_gather(mean_gains, ("section", "tensor"), axis=0, tiled=True)
    shared_gain = all_gains.reshape(groups, rows_dev)[source_pos].reshape(groups * rows_dev)
    device = lax.axis_index(("section", "tensor"))
    seven = jnp.full((1,), 7919, jnp.int32)
    arrived = lax.all_to_all(
        folded.reshape(rows_dev, groups, cols_dev),
        ("section", "tensor"),
        split_axis=1,
        concat_axis=0,
        tiled=True,
    )
    width_cols = arrived.shape[2]
    ordered = arrived.reshape(groups, rows_dev, width_cols)[source_pos].reshape(
        groups * rows_dev, width_cols
    )
    sketches = sketch(ordered, probe_seeds)
    column_probe = probe_at(seven, device * cols_dev + lax.iota(jnp.int32, cols_dev))[0]
    partial_print = jnp.dot(sketches, column_probe, precision=lax.Precision.HIGHEST)
    fingerprint = lax.psum(partial_print, ("section", "tensor")) * FF ** (-0.5)
    return (ordered[None], sketches[None], fingerprint[None], shared_gain)


def solution(mesh):
    return jax.shard_map(
        local,
        mesh=mesh,
        in_specs=(
            P("expert", ("section", "tensor"), None),
            P("expert", ("section", "tensor")),
            P("expert", None),
            P(),
            P(),
        ),
        out_specs=(
            P("expert", None, ("section", "tensor")),
            P("expert", None, ("section", "tensor")),
            P("expert", None),
            P(),
        ),
        check_vma=False,
    )
```

profile of v0, /device:TPU:0, one launch (start us, length us, event | category | flops | bytes accessed | tf_op | source)
XLA Modules:
  0.0 383.8 jit_solution(6322284176018858667)
XLA Ops:
  0.6 6.0 %psum.14 = f32[512]{0:T(512)S(1)} all-reduce(f32[512]{0:T(512)} %bitcast.67), channel_id=1, replica_groups=mesh['section'=4,'expert'=2,'tensor'=4] {'expert'}, use_global_device_ids=true, to_apply=%region_0.0 | all-reduce | flops 512 | bytes 4096 | tf_op jit(solution)/shard_map/psum | solution.py:38
  6.6 0.7 broadcast_multiply_fusion.1
  7.3 11.9 %copy.16 = bf16[1,512,8192]{1,2,0:T(8,128)(2,1)} copy(bf16[1,512,8192]{2,1,0:T(8,128)(2,1)} %param.5) | data formatting | bytes 16777216 | tf_op args[0]
  19.3 0.0 copy-done.1
  19.3 38.2 %gather_fusion = bf16[8192,512]{1,0:T(8,128)(2,1)} fusion(bf16[512,8192]{0,1:T(8,128)(2,1)} %bitcast.48, s32[8192]{0:T(1024)S(1)} %broadcast_clamp_fusion), kind=kCustom, calls=%fused_computation | custom fusion | bytes 16809984 | tf_op jit(solution)/shard_map/jit(_take)/gather | solution.py:40
  57.6 12.3 %copy.17 = bf16[512,16,512]{2,0,1:T(8,128)(2,1)} copy(bf16[512,16,512]{0,2,1:T(8,128)(2,1)} %bitcast.49) | data formatting | bytes 16777216 | tf_op jit(solution)/shard_map/jit(_take)/gather | solution.py:40
  69.8 0.5 broadcast.368
  70.3 0.7 reduce.3
  71.1 9.0 %multiply_convert_fusion = bf16[512,16,512]{2,0,1:T(8,128)(2,1)} fusion(f32[512]{0:T(512)S(1)} %get-tuple-element.13, bf16[512,16,512]{2,0,1:T(8,128)(2,1)} %copy.17, pred[16,512]{1,0:T(8,128)(4,1)S(1)} %compare_and_fusion), kind=kLoop, calls=%fused_computation.3 | loop fusion | flops 16777216 | bytes 16787456 | tf_op jit(solution)/shard_map/convert_element_type | solution.py:41
  80.1 6.7 %all-to-all-start = ((bf16[512,16,512]{2,0,1:T(8,128)(2,1)}), bf16[512,16,512]{2,0,1:T(8,128)(2,1)}, u32[]{:S(2)}, u32[]{:S(2)}) async-start(bf16[512,16,512]{2,0,1:T(8,128)(2,1)} %multiply_convert_fusion), calls=%async_computation | async-start | bytes 16777216 | tf_op jit(solution)/shard_map/all_to_all | solution.py:58
  86.7 207.0 %all-gather = f32[16,1,512]{2,1,0:T(1,128)S(1)} all-gather(f32[1,1,512]{2,1,0:T(1,128)S(1)} %bitcast.66), channel_id=1, replica_groups=mesh['section'=4,'expert'=2,'tensor'=4] {'section','tensor'}, dimensions={0}, use_global_device_ids=true | all-gather | bytes 34816 | tf_op jit(solution)/shard_map/all_gather | solution.py:54
  293.7 0.0 copy-done.3
  293.7 0.1 select_reduce_fusion.1
  293.9 0.1 select_reduce_fusion
  294.0 0.6 gather_fusion.2
  294.5 0.6 copy.19
  295.3 0.0 all-to-all-done
  295.3 8.3 %gather_fusion.1 = bf16[16,512,512]{2,1,0:T(8,128)(2,1)} fusion(bf16[16,512,512]{2,1,0:T(8,128)(2,1)} %bitcast.8, s32[1024]{0:T(1024)S(1)} %pad_clamp_fusion), kind=kCustom, calls=%fused_computation.1 | custom fusion | bytes 16777280 | tf_op jit(solution)/shard_map/gather | solution.py:66
  303.6 4.1 %fusion.212 = (bf16[2,512,512]{2,1,0:T(8,128)(2,1)S(1)}, bf16[2,512,512]{2,1,0:T(8,128)(2,1)S(1)}, bf16[2,512,512]{2,1,0:T(8,128)(2,1)S(1)}, bf16[2,512,512]{2,1...) fusion(bf16[16,512,512]{2,1,0:T(8,128)(2,1)} %gather_fusion.1), kind=kLoop, calls=%fused_computation.260 | loop fusion | bytes 16777216 | tf_op jit(solution)/shard_map/slice | solution.py:23
  307.7 5.3 %fusion.100 = f32[1024,512]{1,0:T(8,128)S(1)} fusion(bf16[1024,512]{1,0:T(8,128)(2,1)S(1)} %bitcast.60, s32[1024]{0:T(1024)S(1)} %iota_add_fusion.6, s32[1024]{0:T(1024)S(1)} %copy-done.2), kind=kOutput, calls=%fused_computation.122 | convolution fusion | flops 1091567616 | bytes 3153920 | tf_op jit(solution)/shard_map/dot_general | solution.py:21
  313.0 5.3 %fusion.88 = f32[1024,512]{1,0:T(8,128)S(1)} fusion(bf16[1024,512]{1,0:T(8,128)(2,1)S(1)} %bitcast.59, s32[1024]{0:T(1024)S(1)} %iota_add_fusion, s32[1024]{0:T(1024)S(1)} %copy-done.2), kind=kOutput, calls=%fused_computation.116 | convolution fusion | flops 1091567616 | bytes 3153920 | tf_op jit(solution)/shard_map/dot_general | solution.py:21
  318.3 5.5 %fusion.90 = f32[1024,512]{1,0:T(8,128)S(1)} fusion(bf16[1024,512]{1,0:T(8,128)(2,1)S(1)} %bitcast.58, s32[1024]{0:T(1024)S(1)} %iota_add_fusion.1, s32[1024]{0:T(1024)S(1)} %copy-done.2), kind=kOutput, calls=%fused_computation.117 | convolution fusion | flops 1091567616 | bytes 3153920 | tf_op jit(solution)/shard_map/dot_general | solution.py:21
  323.7 5.3 %fusion.92 = f32[1024,512]{1,0:T(8,128)S(1)} fusion(bf16[1024,512]{1,0:T(8,128)(2,1)S(1)} %bitcast.57, s32[1024]{0:T(1024)S(1)} %iota_add_fusion.2, s32[1024]{0:T(1024)S(1)} %copy-done.2), kind=kOutput, calls=%fused_computation.118 | convolution fusion | flops 1091567616 | bytes 3153920 | tf_op jit(solution)/shard_map/dot_general | solution.py:21
  329.0 5.7 %fusion.94 = f32[1024,512]{1,0:T(8,128)S(1)} fusion(bf16[1024,512]{1,0:T(8,128)(2,1)S(1)} %bitcast.56, s32[1024]{0:T(1024)S(1)} %iota_add_fusion.3, s32[1024]{0:T(1024)S(1)} %copy-done.2), kind=kOutput, calls=%fused_computation.119 | convolution fusion | flops 1091567616 | bytes 3153920 | tf_op jit(solution)/shard_map/dot_general | solution.py:21
  334.7 5.3 %fusion.96 = f32[1024,512]{1,0:T(8,128)S(1)} fusion(bf16[1024,512]{1,0:T(8,128)(2,1)S(1)} %bitcast.55, s32[1024]{0:T(1024)S(1)} %iota_add_fusion.4, s32[1024]{0:T(1024)S(1)} %copy-done.2), kind=kOutput, calls=%fused_computation.120 | convolution fusion | flops 1091567616 | bytes 3153920 | tf_op jit(solution)/shard_map/dot_general | solution.py:21
  340.0 5.5 %fusion.98 = f32[1024,512]{1,0:T(8,128)S(1)} fusion(bf16[1024,512]{1,0:T(8,128)(2,1)S(1)} %bitcast.54, s32[1024]{0:T(1024)S(1)} %iota_add_fusion.5, s32[1024]{0:T(1024)S(1)} %copy-done.2), kind=kOutput, calls=%fused_computation.121 | convolution fusion | flops 1091567616 | bytes 3153920 | tf_op jit(solution)/shard_map/dot_general | solution.py:21
  345.5 6.0 %add_add_fusion = f32[1024,512]{1,0:T(8,128)S(1)} fusion(f32[1024,512]{1,0:T(8,128)S(1)} %fusion.88, f32[1024,512]{1,0:T(8,128)S(1)} %fusion.90, f32[1024,512]{1,0:T(8,128)S(1)} %fusion.92, f32[1024,512]{1,0:T(8,128)S(1)} %fusion.94, f32[1024,512]{1,0:T(8,128)S(1)} %fusion.96, f32[1024,512]{1,0:T(8,128)S(1)} %fusion.98, f32[1024,512]{1,0:T(8,128)S(1)} %fusion.100, ...), kind=kOutput, calls=%fused_computation.125 | convolution fusion | flops 1095237632 | bytes 17833984 | tf_op jit(solution)/shard_map/dot_general | solution.py:21
  351.5 0.0 copy-start
  351.5 1.9 fusion.213
  353.4 29.7 %psum.15 = f32[1024]{0:T(1024)S(1)} all-reduce(f32[1024]{0:T(1024)S(1)} %bitcast.64), channel_id=1, replica_groups=mesh['section'=4,'expert'=2,'tensor'=4] {'section','tensor'}, use_global_device_ids=true, to_apply=%region_3.4 | all-reduce | flops 1024 | bytes 8192 | tf_op jit(solution)/shard_map/psum | solution.py:72
  383.1 0.6 broadcast_multiply_fusion
  383.7 0.0 copy-done
  (21 shorter events, 0.2 us)
Async XLA Ops:
  7.3 11.9 %copy-start.1 = (s32[1,8192]{1,0:T(1,128)S(1)}, s32[1,8192]{1,0:T(1,128)}, u32[]{:S(2)}) copy-start(s32[1,8192]{1,0:T(1,128)} %param.7) | copy-start | bytes 98308
  80.1 213.7 %copy-start.3 = (s32[4]{0:T(128)S(1)}, s32[4]{0:T(128)}, u32[]{:S(2)}) copy-start(s32[4]{0:T(128)} %param.8) | copy-start | bytes 52
  80.1 215.2 %all-to-all-start = ((bf16[512,16,512]{2,0,1:T(8,128)(2,1)}), bf16[512,16,512]{2,0,1:T(8,128)(2,1)}, u32[]{:S(2)}, u32[]{:S(2)}) async-start(bf16[512,16,512]{2,0,1:T(8,128)(2,1)} %multiply_convert_fusion), calls=%async_computation | async-start | bytes 16777216 | tf_op jit(solution)/shard_map/all_to_all | solution.py:58
  303.6 4.1 %copy-start.2 = (s32[1024]{0:T(1024)S(1)}, s32[1024]{0:T(1024)}, u32[]{:S(2)}) copy-start(s32[1024]{0:T(1024)} %param.9) | copy-start | bytes 12292
  351.5 32.2 %copy-start = (f32[1024,512]{1,0:T(8,128)}, f32[1024,512]{1,0:T(8,128)S(1)}, u32[]{:S(2)}) copy-start(f32[1024,512]{1,0:T(8,128)S(1)} %add_add_fusion) | copy-start | bytes 6291460
where the time goes:
time: 390 us; the launch traced here: 384 us
  blocking collectives  243 us (62%)
  local copies, waits for them, and re-layouts  76.6 us (20%)
  matrix products  45.7 us (12%)
  other arithmetic  11.3 us (3%)
  starting transfers between devices  6.66 us (2%)
    all_gather x1, blocking collectives, local(): lax.all_gather(mean_gains, ('section', 'tensor'), axis=0, tiled=True)  207 us
    gather x2, local copies, waits for them, and re-layouts, local(): permuted = jnp.take(weights, column_order[0], axis=1)  50.5 us
    dot_general x8, matrix products, sketch(): jnp.dot(probes, natural[portion * segment_rows:(portion + 1) * segment_ro...  43.8 us
    psum x1, blocking collectives, local(): fingerprint = lax.psum(partial_print, ('section', 'tensor')) * FF ** (-0.5)  29.7 us
    unnamed x12, local copies, waits for them, and re-layouts  13.1 us
    convert_element_type x1, other arithmetic, local(): (permuted.astype(jnp.float32) * scaling[:, None]).astype(jnp.bfloat16)  8.97 us
    gather x1, local copies, waits for them, and re-layouts, local(): arrived.reshape(groups, rows_dev, width_cols)[source_pos]  8.32 us
  transfers between devices with their start and end apart: 1, of which 0 were waited for; matrix products, arithmetic and copies ran while one was open for 0% of the time, Pallas kernels for 0%

commit v1 on v0

--- a/solution.py
+++ b/solution.py
@@ -51,7 +51,15 @@
         * per_layer
         + block_ids % per_layer
     )
-    all_gains = lax.all_gather(mean_gains, ("section", "tensor"), axis=0, tiled=True)
+    all_gains = jnp.concatenate(
+        lax.all_to_all(
+            jnp.stack([mean_gains] * lax.axis_size(("section", "tensor"))),
+            ("section", "tensor"),
+            0,
+            0,
+        ),
+        axis=0,
+    )
     shared_gain = all_gains.reshape(groups, rows_dev)[source_pos].reshape(groups * rows_dev)
     device = lax.axis_index(("section", "tensor"))
     seven = jnp.full((1,), 7919, jnp.int32)

time: 390 us -> 374 us (0.959)
  blocking collectives: 243 us -> 37.4 us
  waiting for transfers between devices: 0.01 us -> 183 us
  starting transfers between devices: 6.66 us -> 12.7 us
    all_gather x1 -> x0, blocking collectives: 207 us -> none  [local(): lax.all_gather(mean_gains, ('section', 'tensor'), axis=0, tiled=True)]
    all_to_all x1, waiting for transfers between devices: 0.01 us -> 183 us  [local(): lax.all_to_all(folded.reshape(rows_dev, groups, cols_dev), ('section', 't...]
    all_to_all x0 -> x1, starting transfers between devices: none -> 6.48 us  [local(): lax.all_to_all(jnp.stack([mean_gains] * lax.axis_size(('section', 'tensor...]
  transfers between devices with their start and end apart: 1 -> 2, of which waited for: 0 -> 1; matrix products, arithmetic and copies ran while one was open for 0% -> 20% of each run, Pallas kernels for 0% -> 0%
where the time goes in v1:
time: 374 us; the launch traced here: 368 us
  waiting for transfers between devices  183 us (49%)
  local copies, waits for them, and re-layouts  77.2 us (21%)
  matrix products  45.7 us (12%)
  blocking collectives  37.4 us (10%)
  starting transfers between devices  12.7 us (3%)
  other arithmetic  11.3 us (3%)
    all_to_all x1, waiting for transfers between devices, local(): lax.all_to_all(folded.reshape(rows_dev, groups, cols_dev), ('section', 't...  183 us
    gather x2, local copies, waits for them, and re-layouts, local(): permuted = jnp.take(weights, column_order[0], axis=1)  50.5 us
    dot_general x8, matrix products, sketch(): jnp.dot(probes, natural[portion * segment_rows:(portion + 1) * segment_ro...  43.8 us
    psum x1, blocking collectives, local(): fingerprint = lax.psum(partial_print, ('section', 'tensor')) * FF ** (-0.5)  31.4 us
    unnamed x12, local copies, waits for them, and re-layouts  13.1 us
    convert_element_type x1, other arithmetic, local(): (permuted.astype(jnp.float32) * scaling[:, None]).astype(jnp.bfloat16)  8.97 us
    gather x1, local copies, waits for them, and re-layouts, local(): arrived.reshape(groups, rows_dev, width_cols)[source_pos]  8.32 us
  transfers between devices with their start and end apart: 2, of which 1 were waited for; matrix products, arithmetic and copies ran while one was open for 20% of the time, Pallas kernels for 0%

profile of v1, /device:TPU:0, one launch (start us, length us, event | category | flops | bytes accessed | tf_op | source)
XLA Modules:
  0.0 367.8 jit_solution(7823173047653040114)
XLA Ops:
  0.6 6.0 %psum.14 = f32[512]{0:T(512)S(1)} all-reduce(f32[512]{0:T(512)} %bitcast.65), channel_id=1, replica_groups=mesh['section'=4,'expert'=2,'tensor'=4] {'expert'}, use_global_device_ids=true, to_apply=%region_0.0 | all-reduce | flops 512 | bytes 4096 | tf_op jit(solution)/shard_map/psum | solution.py:38
  6.6 0.7 broadcast_multiply_fusion.1
  7.3 0.6 stack.2
  8.0 6.5 %all-to-all-start.1 = ((f32[16,1,512]{2,1,0:T(1,128)}), f32[16,1,512]{2,1,0:T(1,128)S(1)}, u32[]{:S(2)}, u32[]{:S(2)}) async-start(f32[16,1,512]{2,1,0:T(1,128)} %stack.2), calls=%async_computation.1 | async-start | bytes 65536 | tf_op jit(solution)/shard_map/all_to_all | solution.py:55
  14.4 0.0 copy-start.1
  14.5 11.9 %copy.16 = bf16[1,512,8192]{1,2,0:T(8,128)(2,1)} copy(bf16[1,512,8192]{2,1,0:T(8,128)(2,1)} %param.5) | data formatting | bytes 16777216 | tf_op args[0]
  26.4 38.2 %gather_fusion = bf16[8192,512]{1,0:T(8,128)(2,1)} fusion(bf16[512,8192]{0,1:T(8,128)(2,1)} %bitcast.47, s32[8192]{0:T(1024)S(1)} %broadcast_clamp_fusion), kind=kCustom, calls=%fused_computation | custom fusion | bytes 16809984 | tf_op jit(solution)/shard_map/jit(_take)/gather | solution.py:40
  64.7 12.3 %copy.17 = bf16[512,16,512]{2,0,1:T(8,128)(2,1)} copy(bf16[512,16,512]{0,2,1:T(8,128)(2,1)} %bitcast.48) | data formatting | bytes 16777216 | tf_op jit(solution)/shard_map/jit(_take)/gather | solution.py:40
  76.9 0.5 broadcast.372
  77.5 0.7 reduce.3
  78.2 9.0 %multiply_convert_fusion = bf16[512,16,512]{2,0,1:T(8,128)(2,1)} fusion(f32[512]{0:T(512)S(1)} %get-tuple-element.13, bf16[512,16,512]{2,0,1:T(8,128)(2,1)} %copy.17, pred[16,512]{1,0:T(8,128)(4,1)S(1)} %compare_and_fusion), kind=kLoop, calls=%fused_computation.3 | loop fusion | flops 16777216 | bytes 16787456 | tf_op jit(solution)/shard_map/convert_element_type | solution.py:41
  87.2 0.0 all-to-all-done.1
  87.2 6.2 %all-to-all-start = ((bf16[512,16,512]{2,0,1:T(8,128)(2,1)}), bf16[512,16,512]{2,0,1:T(8,128)(2,1)}, u32[]{:S(2)}, u32[]{:S(2)}) async-start(bf16[512,16,512]{2,0,1:T(8,128)(2,1)} %multiply_convert_fusion), calls=%async_computation | async-start | bytes 16777216 | tf_op jit(solution)/shard_map/all_to_all | solution.py:66
  93.5 0.1 select_reduce_fusion.1
  93.6 0.1 select_reduce_fusion
  93.8 0.6 gather_fusion.2
  94.3 0.6 copy.19
  95.0 182.6 %all-to-all-done = bf16[512,16,512]{2,0,1:T(8,128)(2,1)} async-done(((bf16[512,16,512]{2,0,1:T(8,128)(2,1)}), bf16[512,16,512]{2,0,1:T(8,128)(2,1)}, u32[]{:S(2)}, u32[]{:S(2)}) %all-to-all-start) | async-done | bytes 8388640 | tf_op jit(solution)/shard_map/all_to_all | solution.py:66
  277.6 8.3 %gather_fusion.1 = bf16[16,512,512]{2,1,0:T(8,128)(2,1)} fusion(bf16[16,512,512]{2,1,0:T(8,128)(2,1)} %bitcast.8, s32[1024]{0:T(1024)S(1)} %pad_clamp_fusion), kind=kCustom, calls=%fused_computation.1 | custom fusion | bytes 16777280 | tf_op jit(solution)/shard_map/gather | solution.py:74
  285.9 4.1 %fusion.212 = (bf16[2,512,512]{2,1,0:T(8,128)(2,1)S(1)}, bf16[2,512,512]{2,1,0:T(8,128)(2,1)S(1)}, bf16[2,512,512]{2,1,0:T(8,128)(2,1)S(1)}, bf16[2,512,512]{2,1...) fusion(bf16[16,512,512]{2,1,0:T(8,128)(2,1)} %gather_fusion.1), kind=kLoop, calls=%fused_computation.260 | loop fusion | bytes 16777216 | tf_op jit(solution)/shard_map/slice | solution.py:23
  290.0 5.3 %fusion.100 = f32[1024,512]{1,0:T(8,128)S(1)} fusion(bf16[1024,512]{1,0:T(8,128)(2,1)S(1)} %bitcast.59, s32[1024]{0:T(1024)S(1)} %iota_add_fusion.6, s32[1024]{0:T(1024)S(1)} %copy-done.2), kind=kOutput, calls=%fused_computation.122 | convolution fusion | flops 1091567616 | bytes 3153920 | tf_op jit(solution)/shard_map/dot_general | solution.py:21
  295.3 5.3 %fusion.88 = f32[1024,512]{1,0:T(8,128)S(1)} fusion(bf16[1024,512]{1,0:T(8,128)(2,1)S(1)} %bitcast.58, s32[1024]{0:T(1024)S(1)} %iota_add_fusion, s32[1024]{0:T(1024)S(1)} %copy-done.2), kind=kOutput, calls=%fused_computation.116 | convolution fusion | flops 1091567616 | bytes 3153920 | tf_op jit(solution)/shard_map/dot_general | solution.py:21
  300.5 5.5 %fusion.90 = f32[1024,512]{1,0:T(8,128)S(1)} fusion(bf16[1024,512]{1,0:T(8,128)(2,1)S(1)} %bitcast.57, s32[1024]{0:T(1024)S(1)} %iota_add_fusion.1, s32[1024]{0:T(1024)S(1)} %copy-done.2), kind=kOutput, calls=%fused_computation.117 | convolution fusion | flops 1091567616 | bytes 3153920 | tf_op jit(solution)/shard_map/dot_general | solution.py:21
  306.0 5.3 %fusion.92 = f32[1024,512]{1,0:T(8,128)S(1)} fusion(bf16[1024,512]{1,0:T(8,128)(2,1)S(1)} %bitcast.56, s32[1024]{0:T(1024)S(1)} %iota_add_fusion.2, s32[1024]{0:T(1024)S(1)} %copy-done.2), kind=kOutput, calls=%fused_computation.118 | convolution fusion | flops 1091567616 | bytes 3153920 | tf_op jit(solution)/shard_map/dot_general | solution.py:21
  311.3 5.7 %fusion.94 = f32[1024,512]{1,0:T(8,128)S(1)} fusion(bf16[1024,512]{1,0:T(8,128)(2,1)S(1)} %bitcast.55, s32[1024]{0:T(1024)S(1)} %iota_add_fusion.3, s32[1024]{0:T(1024)S(1)} %copy-done.2), kind=kOutput, calls=%fused_computation.119 | convolution fusion | flops 1091567616 | bytes 3153920 | tf_op jit(solution)/shard_map/dot_general | solution.py:21
  317.0 5.3 %fusion.96 = f32[1024,512]{1,0:T(8,128)S(1)} fusion(bf16[1024,512]{1,0:T(8,128)(2,1)S(1)} %bitcast.54, s32[1024]{0:T(1024)S(1)} %iota_add_fusion.4, s32[1024]{0:T(1024)S(1)} %copy-done.2), kind=kOutput, calls=%fused_computation.120 | convolution fusion | flops 1091567616 | bytes 3153920 | tf_op jit(solution)/shard_map/dot_general | solution.py:21
  322.3 5.5 %fusion.98 = f32[1024,512]{1,0:T(8,128)S(1)} fusion(bf16[1024,512]{1,0:T(8,128)(2,1)S(1)} %bitcast.53, s32[1024]{0:T(1024)S(1)} %iota_add_fusion.5, s32[1024]{0:T(1024)S(1)} %copy-done.2), kind=kOutput, calls=%fused_computation.121 | convolution fusion | flops 1091567616 | bytes 3153920 | tf_op jit(solution)/shard_map/dot_general | solution.py:21
  327.7 6.0 %add_add_fusion = f32[1024,512]{1,0:T(8,128)S(1)} fusion(f32[1024,512]{1,0:T(8,128)S(1)} %fusion.88, f32[1024,512]{1,0:T(8,128)S(1)} %fusion.90, f32[1024,512]{1,0:T(8,128)S(1)} %fusion.92, f32[1024,512]{1,0:T(8,128)S(1)} %fusion.94, f32[1024,512]{1,0:T(8,128)S(1)} %fusion.96, f32[1024,512]{1,0:T(8,128)S(1)} %fusion.98, f32[1024,512]{1,0:T(8,128)S(1)} %fusion.100, ...), kind=kOutput, calls=%fused_computation.125 | convolution fusion | flops 1095237632 | bytes 17833984 | tf_op jit(solution)/shard_map/dot_general | solution.py:21
  333.8 0.0 copy-start
  333.8 1.9 fusion.213
  335.6 31.4 %psum.15 = f32[1024]{0:T(1024)S(1)} all-reduce(f32[1024]{0:T(1024)S(1)} %bitcast.63), channel_id=1, replica_groups=mesh['section'=4,'expert'=2,'tensor'=4] {'section','tensor'}, use_global_device_ids=true, to_apply=%region_3.4 | all-reduce | flops 1024 | bytes 8192 | tf_op jit(solution)/shard_map/psum | solution.py:80
  367.0 0.6 broadcast_multiply_fusion
  (23 shorter events, 0.2 us)
Async XLA Ops:
  8.0 79.2 %all-to-all-start.1 = ((f32[16,1,512]{2,1,0:T(1,128)}), f32[16,1,512]{2,1,0:T(1,128)S(1)}, u32[]{:S(2)}, u32[]{:S(2)}) async-start(f32[16,1,512]{2,1,0:T(1,128)} %stack.2), calls=%async_computation.1 | async-start | bytes 65536 | tf_op jit(solution)/shard_map/all_to_all | solution.py:55
  14.4 12.0 %copy-start.1 = (s32[1,8192]{1,0:T(1,128)S(1)}, s32[1,8192]{1,0:T(1,128)}, u32[]{:S(2)}) copy-start(s32[1,8192]{1,0:T(1,128)} %param.7) | copy-start | bytes 98308
  87.2 6.3 %copy-start.3 = (s32[4]{0:T(128)S(1)}, s32[4]{0:T(128)}, u32[]{:S(2)}) copy-start(s32[4]{0:T(128)} %param.8) | copy-start | bytes 52
  87.2 190.4 %all-to-all-start = ((bf16[512,16,512]{2,0,1:T(8,128)(2,1)}), bf16[512,16,512]{2,0,1:T(8,128)(2,1)}, u32[]{:S(2)}, u32[]{:S(2)}) async-start(bf16[512,16,512]{2,0,1:T(8,128)(2,1)} %multiply_convert_fusion), calls=%async_computation | async-start | bytes 16777216 | tf_op jit(solution)/shard_map/all_to_all | solution.py:66
  285.9 4.1 %copy-start.2 = (s32[1024]{0:T(1024)S(1)}, s32[1024]{0:T(1024)}, u32[]{:S(2)}) copy-start(s32[1024]{0:T(1024)} %param.9) | copy-start | bytes 12292
  333.8 33.8 %copy-start = (f32[1024,512]{1,0:T(8,128)}, f32[1024,512]{1,0:T(8,128)S(1)}, u32[]{:S(2)}) copy-start(f32[1024,512]{1,0:T(8,128)S(1)} %add_add_fusion) | copy-start | bytes 6291460
